TPU v7x, 128 devices: a whole 4x4x4 slice. The times are simulated.
128 devices in a mesh: gz: 128 (over y, z, x, core).
Axes of the slice: x: 4, y: 4, z: 4, core: 2. Of those that a mesh axis runs over, the one named last changes fastest.
Arguments:
- scores: int32 [512, 512, 512], P('gz'), may hold values from 0 to 134217727, as said below
Outputs:
- status: int32 [512, 512, 512], P('gz')
- counts: int32 [3], replicated
Inputs may be any that keep to these rules, and one draw needn't show every extreme that they name: `scores`: all values distinct: a permutation of 0 to 134217727.
All inputs are finite; a program needn't handle non-finite values.
Results may differ from a plain program's by a relative error of at most 0.000001.
Values may be sent and summed in bfloat16 or wider, within the bound.
A program may use at most 64 MiB of HBM per device.

v0:
```python
import functools

import jax
import jax.numpy as jnp
from jax import lax
from jax.experimental import pallas as pl
from jax.experimental.pallas import tpu as pltpu
from jax.sharding import PartitionSpec as P


AXIS = "gz"
FINE = 32
ROWS = 64
PARTS = 4
PAD = 8
LANES = 128
NONE = -(2.0**126)


def roll(x, shift, axis):
    return pltpu.roll(x, shift % x.shape[axis], axis)


def encode(score, total):
    if total <= 1 << 25:
        return (score - (1 << 24)).astype(jnp.float32)
    value = ((score & ((1 << 23) - 1)) + (1 << 23)).astype(jnp.float32)
    for bit in range(23, (total - 1).bit_length()):
        factor = jnp.where((score & (1 << bit)) != 0, 2.0 ** (1 << (bit - 23)), 1.0)
        value = value * factor
    return value


def spread(load, chunks, op, blank, lane):
    x = [
        op(
            op(op(load(c, -2), load(c, -1)), op(load(c, 0), load(c, 1))),
            load(c, 2),
        )
        for c in range(chunks)
    ]
    one = [roll(v, -1, 1) for v in x] + [blank]
    two = [roll(v, -2, 1) for v in x] + [blank]
    pair = [
        op(x[c], jnp.where(lane >= LANES - 1, one[c + 1], one[c])) for c in range(chunks)
    ]
    before = [jnp.where(lane == 1, roll(x[0], 1, 1), blank)]
    before += [roll(v, 2, 1) for v in pair]
    return [
        op(
            op(pair[c], jnp.where(lane < 2, before[c], before[c + 1])),
            jnp.where(lane >= LANES - 2, two[c + 1], two[c]),
        )
        for c in range(chunks)
    ]


def parity():
    row = lax.broadcasted_iota(jnp.int32, (8, LANES), 0) % 2 == 0
    lane = lax.broadcasted_iota(jnp.int32, (8, LANES), 1) % 2 == 0
    return row, lane


def pack(x):
    row, lane = parity()
    half = len(x) // 2

    def fold(part):
        part = jnp.maximum(part, roll(part, -1, 0))
        return jnp.maximum(part, roll(part, -1, 1))

    out = []
    for c in range(half):
        rows = []
        for r in range(0, x[0].shape[0], 16):
            quads = [
                jnp.where(
                    lane, fold(x[c][k : k + 8]), roll(fold(x[c + half][k : k + 8]), 1, 1)
                )
                for k in (r, r + 8)
            ]
            rows.append(jnp.where(row, quads[0], roll(quads[1], 1, 0)))
        out.append(jnp.concatenate(rows, axis=0))
    return out


def unpack(x):
    row, lane = parity()
    low, high = [], []
    for v in x:
        lows, highs = [], []
        for r in range(0, v.shape[0], 8):
            part = v[r : r + 8]
            for rows in (
                jnp.where(row, part, roll(part, 1, 0)),
                jnp.where(row, roll(part, -1, 0), part),
            ):
                lows.append(jnp.where(lane, rows, roll(rows, 1, 1)))
                highs.append(jnp.where(lane, roll(rows, -1, 1), rows))
        low.append(jnp.concatenate(lows, axis=0))
        high.append(jnp.concatenate(highs, axis=0))
    return low + high


def kernel(
    n, scores, packed_status, counts, field, near, bits, found, cand_send, cand_recv,
    resp_send, resp_recv, tally, cnt_send, cnt_recv, send_sem, recv_sem,
    cnt_send_sem, cnt_recv_sem,
):
    depth, nx, ny = scores.shape
    total = n * depth * nx * ny
    chunks = ny // LANES
    me = lax.axis_index(AXIS)
    has = (me > 0, me < n - 1)
    lone = tuple(jnp.where(h, 0, 1).astype(jnp.int32) for h in has)
    edge = ((0, 1), (depth - 2, depth - 1))
    halo_bits = ((0, 1), (depth + 2, depth + 3))
    lane = lax.broadcasted_iota(jnp.int32, (FINE, LANES), 1)

    def spot(rows):
        shape = (rows, LANES)
        row = lax.broadcasted_iota(jnp.int32, shape, 0) % 2
        return row * 2 + lax.broadcasted_iota(jnp.int32, shape, 1) % 2

    part_rows = nx // PARTS
    columns = [slice(c * LANES, (c + 1) * LANES) for c in range(chunks)]

    barrier = pltpu.get_barrier_semaphore()

    @pl.loop(1, n)
    def _(i):
        pl.semaphore_signal(
            barrier,
            inc=1,
            device_id=(lax.rem(me + i, n),),
            device_id_type=pl.DeviceIdType.MESH,
        )

    for rows in (slice(0, PAD), slice(PAD + nx, 2 * PAD + nx)):
        field[:, :, rows, :] = jnp.full((depth, chunks, PAD, LANES), NONE, jnp.float32)
        bits[:, rows, :] = jnp.zeros((chunks, PAD, LANES), jnp.int32)
    tally[...] = jnp.zeros_like(tally)
    for side in range(2):

        @pl.when(jnp.logical_not(has[side]))
        def _():
            for phase in range(2):
                cand_recv[phase, side] = jnp.full(cand_recv.shape[2:], -1, jnp.int32)
                resp_recv[phase, side] = jnp.ones(resp_recv.shape[2:], jnp.bfloat16)

    @pl.loop(0, nx // ROWS)
    def _(block):
        top = pl.multiple_of(block * ROWS, ROWS)
        for z in range(depth):
            for c in range(chunks):
                field[z, c, pl.ds(pl.multiple_of(top + PAD, PAD), ROWS), :] = encode(
                    scores[z, pl.ds(top, ROWS), columns[c]], total
                )

    pl.semaphore_wait(barrier, n - 1)

    def exchange(send, recv, phase, step, side, part, arrival):
        rows = pl.ds(pl.multiple_of(part * (part_rows // 2), part_rows // 2), part_rows // 2)
        there = arrival if arrival is not None else 1 - side
        return pltpu.make_async_remote_copy(
            src_ref=send.at[phase, side, rows, :],
            dst_ref=recv.at[phase, there, rows, :],
            send_sem=send_sem.at[step, side, part],
            recv_sem=recv_sem.at[step, there, part],
            device_id=(me + (1 if side else -1),),
            device_id_type=pl.DeviceIdType.MESH,
        )

    def start(send, recv, phase, step, part):
        for side in range(2):

            @pl.when(has[side])
            def _():
                exchange(send, recv, phase, step, side, part, None).start()

    def finish(send, recv, phase, step, part):
        for side in range(2):

            @pl.when(has[side])
            def _():
                exchange(send, recv, phase, step, side, part, None).wait_send()
                exchange(send, recv, phase, step, side, part, side).wait_recv()

    def search(phase, part):
        place = spot(FINE)

        @pl.loop(0, part_rows // FINE)
        def _(block):
            top = pl.multiple_of(part * part_rows + block * FINE, FINE)
            here = pl.ds(top, FINE)
            wide = [
                spread(
                    lambda c, d: field[z, c, pl.ds(top + (PAD + d), FINE), :],
                    chunks, jnp.maximum, NONE, lane,
                )
                for z in range(depth)
            ]
            codes = ([], [])
            count = jnp.zeros((FINE, LANES), jnp.int32)
            for c in range(chunks):
                w = [wide[z][c] for z in range(depth)]
                low, high = jnp.maximum(w[0], w[1]), jnp.maximum(w[-1], w[-2])
                near[0, 0, c, here, :] = w[0]
                near[0, 1, c, here, :] = low
                near[1, 0, c, here, :] = high
                near[1, 1, c, here, :] = w[-1]
                own = jnp.zeros((FINE, LANES), jnp.int32)
                best = []
                for z in range(depth):
                    value = field[z, c, pl.ds(pl.multiple_of(top + PAD, PAD), FINE), :]
                    terms = {k: w[k] for k in range(max(z - 2, 0), min(z + 3, depth))}
                    if 0 in terms and 1 in terms:
                        terms[0] = low
                        del terms[1]
                    if depth - 1 in terms and depth - 2 in terms:
                        terms[depth - 1] = high
                        del terms[depth - 2]
                    is_best = value == functools.reduce(jnp.maximum, list(terms.values()))
                    if phase:
                        is_best = is_best & (value > NONE)
                    own = own | jnp.where(is_best, 4 << z, 0)
                    best.append(is_best)
                found[c, here, :] = own
                for side in range(2):
                    a, b = edge[side]
                    held_a = scores[a, here, columns[c]]
                    held_b = scores[b, here, columns[c]]
                    codes[side].append(
                        jnp.where(
                            best[a],
                            held_a * 8 + place,
                            jnp.where(best[b], held_b * 8 + (place + 4), -1),
                        )
                    )
                if phase:
                    for side in range(2):
                        for z in edge[side]:
                            count = count + jnp.where(best[z], lone[side], 0)
                    for z in range(2, depth - 2):
                        count = count + jnp.where(best[z], 1, 0)
            small = pl.ds(pl.multiple_of(top // 2, FINE // 2), FINE // 2)
            for side in range(2):
                for c, v in enumerate(pack(codes[side])):
                    cand_send[phase, side, small, columns[c]] = v
            if phase:
                tally[2, :FINE] += count

    def judge(phase, part):
        place = spot(ROWS)

        @pl.loop(0, part_rows // ROWS)
        def _(block):
            top = pl.multiple_of(part * part_rows + block * ROWS, ROWS)
            small = pl.ds(pl.multiple_of(top // 2, ROWS // 2), ROWS // 2)
            here = pl.ds(top, ROWS)
            halo = [jnp.zeros((ROWS, LANES), jnp.int32) for _ in range(chunks)]
            count = jnp.zeros((ROWS, LANES), jnp.int32)
            for side in range(2):
                codes = unpack(
                    [cand_recv[phase, side, small, columns[c]] for c in range(chunks // 2)]
                )
                verdicts = []
                for c, code in enumerate(codes):
                    where = code & 7
                    score = jnp.where(code < 0, NONE, encode(code >> 3, total))
                    low = (where == place) & (score > near[side, 0, c, here, :])
                    high = (where == place + 4) & (score > near[side, 1, c, here, :])
                    alive = jnp.where(low | high, 1, 0)
                    verdicts.append(alive)
                    if phase:
                        count = count + alive
                    else:
                        halo[c] = halo[c] | jnp.where(low, 1 << halo_bits[side][0], 0)
                        halo[c] = halo[c] | jnp.where(high, 1 << halo_bits[side][1], 0)
                for c, v in enumerate(pack(verdicts)):
                    resp_send[phase, side, small, columns[c]] = v.astype(
                        jnp.float32
                    ).astype(jnp.bfloat16)
            if phase:
                tally[2] += count
            else:
                for c in range(chunks):
                    bits[c, pl.ds(pl.multiple_of(top + PAD, PAD), ROWS), :] = halo[c]

    def confirmed(phase, top):
        small = pl.ds(pl.multiple_of(top // 2, ROWS // 2), ROWS // 2)
        own = [found[c, pl.ds(top, ROWS), :] for c in range(chunks)]
        for side in range(2):
            verdicts = unpack(
                [
                    resp_recv[phase, side, small, columns[c]].astype(jnp.float32)
                    for c in range(chunks // 2)
                ]
            )
            mask = (4 << edge[side][0]) | (4 << edge[side][1])
            own = [jnp.where(v > 0.5, o, o & ~mask) for v, o in zip(verdicts, own)]
        return own

    def settle(part):
        @pl.loop(0, part_rows // ROWS)
        def _(block):
            top = pl.multiple_of(part * part_rows + block * ROWS, ROWS)
            for c, own in enumerate(confirmed(0, top)):
                bits[c, pl.ds(pl.multiple_of(top + PAD, PAD), ROWS), :] |= own

    def remove(part):
        @pl.loop(0, part_rows // FINE)
        def _(block):
            top = pl.multiple_of(part * part_rows + block * FINE, FINE)
            centre = pl.ds(pl.multiple_of(top + PAD, PAD), FINE)
            reach = spread(
                lambda c, d: bits[c, pl.ds(top + (PAD + d), FINE), :],
                chunks, jnp.bitwise_or, 0, lane,
            )
            first, second = tally[0, :FINE], tally[1, :FINE]
            for c in range(chunks):
                roots = bits[c, centre, :]
                status = jnp.zeros((FINE, LANES), jnp.int32)
                for z in range(depth):
                    is_root = (roots & (4 << z)) != 0
                    covered = (reach[c] & (31 << z)) != 0
                    field[z, c, centre, :] = jnp.where(covered, NONE, field[z, c, centre, :])
                    status = status | jnp.where(
                        is_root, 1 << (2 * z), jnp.where(covered, 2 << (2 * z), 0)
                    )
                    first = first + jnp.where(is_root, 1, 0)
                    second = second + jnp.where(covered, 1, 0)
                packed_status[pl.ds(top, FINE), columns[c]] = status
            tally[0, :FINE] = first
            tally[1, :FINE] = second

    def offer(phase, part):
        search(phase, part)
        start(cand_send, cand_recv, phase, 2 * phase, part)

    def answer(phase, part):
        finish(cand_send, cand_recv, phase, 2 * phase, part)
        judge(phase, part)
        start(resp_send, resp_recv, phase, 2 * phase + 1, part)

    @pl.loop(0, PARTS)
    def _(part):
        offer(0, part)

    @pl.loop(0, PARTS)
    def _(part):
        answer(0, part)

    @pl.loop(0, PARTS + 2)
    def _(part):
        @pl.when(part < PARTS)
        def _():
            finish(resp_send, resp_recv, 0, 1, part)
            settle(part)

        @pl.when((part > 0) & (part <= PARTS))
        def _():
            remove(part - 1)

        @pl.when(part > 1)
        def _():
            offer(1, part - 2)

    @pl.loop(0, PARTS)
    def _(part):
        answer(1, part)

    roots, covered, late = (jnp.sum(tally[i]) for i in range(3))
    cells = depth * nx * ny
    column = lax.broadcasted_iota(jnp.int32, cnt_send.shape, 1)
    mine = jnp.where(
        column == 0,
        cells - roots,
        jnp.where(column == 1, cells - covered, cells - covered - late),
    )
    cnt_send[...] = mine

    def report(i):
        return pltpu.make_async_remote_copy(
            src_ref=cnt_send,
            dst_ref=cnt_recv.at[i],
            send_sem=cnt_send_sem.at[i],
            recv_sem=cnt_recv_sem.at[i],
            device_id=(lax.rem(me + i, n),),
            device_id_type=pl.DeviceIdType.MESH,
        )

    @pl.loop(1, n)
    def _(i):
        report(i).start()

    @pl.loop(0, PARTS)
    def _(part):
        finish(resp_send, resp_recv, 1, 3, part)

        @pl.loop(0, part_rows // ROWS)
        def _(block):
            top = pl.multiple_of(part * part_rows + block * ROWS, ROWS)
            for c, own in enumerate(confirmed(1, top)):
                status = packed_status[pl.ds(top, ROWS), columns[c]]
                for z in range(depth):
                    status = status | jnp.where((own & (4 << z)) != 0, 1 << (2 * z), 0)
                packed_status[pl.ds(top, ROWS), columns[c]] = status

    @pl.loop(1, n)
    def _(i):
        report(i).wait()

    cnt_recv[0] = mine
    counts[...] = jnp.sum(cnt_recv[...], axis=0)


def shards(scores):
    depth, nx, ny = scores.shape
    n = lax.axis_size(AXIS)
    vmem = pltpu.VMEM
    small = (nx // 2, ny // 2)
    chunks = ny // LANES
    packed_status, counts = pl.pallas_call(
        functools.partial(kernel, n),
        out_shape=(
            jax.ShapeDtypeStruct((nx, ny), jnp.int32),
            jax.ShapeDtypeStruct((8, 128), jnp.int32),
        ),
        in_specs=[pl.BlockSpec(memory_space=vmem)],
        out_specs=(pl.BlockSpec(memory_space=vmem),) * 2,
        scratch_shapes=[
            vmem((depth, chunks, nx + 2 * PAD, LANES), jnp.float32),
            vmem((2, 2, chunks, nx, LANES), jnp.float32),
            vmem((chunks, nx + 2 * PAD, LANES), jnp.int32),
            vmem((chunks, nx, LANES), jnp.int32),
            vmem((2, 2) + small, jnp.int32),
            vmem((2, 2) + small, jnp.int32),
            vmem((2, 2) + small, jnp.bfloat16),
            vmem((2, 2) + small, jnp.bfloat16),
            vmem((3, ROWS, LANES), jnp.int32),
            vmem((8, 128), jnp.int32),
            vmem((n, 8, 128), jnp.int32),
            pltpu.SemaphoreType.DMA((4, 2, PARTS)),
            pltpu.SemaphoreType.DMA((4, 2, PARTS)),
            pltpu.SemaphoreType.DMA((n,)),
            pltpu.SemaphoreType.DMA((n,)),
        ],
        compiler_params=pltpu.CompilerParams(
            collective_id=0, has_side_effects=True, vmem_limit_bytes=48 * 1024 * 1024
        ),
    )(scores)
    place = 2 * jnp.arange(depth, dtype=jnp.int32)[:, None, None]
    return (packed_status[None] >> place) & 3, counts[0, :3]


def solution(mesh):
    return jax.shard_map(
        shards,
        mesh=mesh,
        in_specs=(P(AXIS, None, None),),
        out_specs=(P(AXIS, None, None), P()),
        check_vma=False,
    )
```

profile of v0, /device:TPU:0, one launch (start us, length us, event | category | flops | bytes accessed | tf_op | source)
XLA Modules:
  0.0 59.7 jit_solution(16908308426354744080)
XLA Ops:
  0.6 0.0 copy-start
  0.7 2.2 %copy-done = s32[4,512,512]{2,1,0:T(8,128)S(1)} copy-done((s32[4,512,512]{2,1,0:T(8,128)S(1)}, s32[4,512,512]{2,1,0:T(8,128)}, u32[]{:S(2)}) %copy-start) | copy-done | bytes 4194328
  2.8 53.7 %shard_map.30 = (s32[512,512]{1,0:T(8,128)S(1)}, s32[8,128]{1,0:T(8,128)S(1)}) custom-call(s32[4,512,512]{2,1,0:T(8,128)S(1)} %copy-done), custom_call_target="tpu_custom_call" | custom-call | tf_op jit(solution)/shard_map/pallas_call | solution.py:424
  56.6 0.5 slice_bitcast_fusion
  57.1 2.6 %shift-right-arithmetic_and_fusion = s32[4,512,512]{2,1,0:T(8,128)} fusion(s32[4]{0:T(128)S(1)} %iota_multiply_fusion, s32[512,512]{1,0:T(8,128)S(1)} %get-tuple-element.4), kind=kLoop, calls=%fused_computation | loop fusion | flops 2097152 | bytes 5242896 | tf_op jit(solution)/shard_map/and | solution.py:454
  (1 shorter events, 0.0 us)
Async XLA Ops:
  0.6 2.2 %copy-start = (s32[4,512,512]{2,1,0:T(8,128)S(1)}, s32[4,512,512]{2,1,0:T(8,128)}, u32[]{:S(2)}) copy-start(s32[4,512,512]{2,1,0:T(8,128)} %scores.1) | copy-start | bytes 12582916
where the time goes:
time: 60.9 us; the launch traced here: 59.7 us
  Pallas kernels  53.7 us (88%)
  local copies, waits for them, and re-layouts  2.7 us (4%)
  other arithmetic  2.64 us (4%)
  between operations  0.65 us (1%)
    pallas_call x1, Pallas kernels, shards(): pl.pallas_call(functools.partial(kernel, n), out_shape=(jax.ShapeDtypeStr...  53.7 us
    and x1, other arithmetic, shards(): return (packed_status[None] >> place & 3, counts[0, :3])  2.64 us
    unnamed x2, local copies, waits for them, and re-layouts  2.18 us

commit v1 on v0

v1 whole, which is shorter than its diff:
```python
import functools
import math

import jax
import jax.numpy as jnp
from jax import lax
from jax.experimental import pallas as pl
from jax.experimental.pallas import tpu as pltpu
from jax.sharding import PartitionSpec as P


AXIS = "gz"
SUB = 8
LANES = 128
PARTS = 4
HALO = 2
GROUP = 8
JUDGED = 4
WIDENED = 8
LOW = 0x0C
HIGH = 0x30


def roll(x, shift, axis):
    return pltpu.roll(x, shift % x.shape[axis], axis)


def lane_index():
    return lax.broadcasted_iota(jnp.int32, (SUB, LANES), 1)


def encode(score):
    value = ((score & ((1 << 23) - 1)) | (1 << 23)).astype(jnp.float32)
    scale = lax.shift_left(jnp.ones_like(score), lax.shift_right_logical(score, 23))
    return value * scale.astype(jnp.float32)


def lanes5(x, op, lane):
    blank = jnp.zeros_like(x[0])
    low, high = op(x[0], x[1]), op(x[2], x[3])
    whole = op(low, high)

    def before(v):
        return jnp.where(lane == 0, blank, roll(v, 1, 1))

    def after(v):
        return jnp.where(lane == LANES - 1, blank, roll(v, -1, 1))

    return [
        op(op(low, x[2]), before(high)),
        op(whole, before(x[3])),
        op(whole, after(x[0])),
        op(op(x[1], high), after(low)),
    ]


def rows5(load, op):
    x = {d: load(d) for d in range(-2, 6)}
    middle = op(x[1], x[2])
    left, right = op(x[0], middle), op(middle, x[3])
    left, right = op(x[-1], left), op(right, x[4])
    return [op(left, x[-2]), op(left, x[3]), op(x[0], right), op(right, x[5])]


def kernel(
    n, scores, packed_status, counts, raw, turned, codes, field, wide, near, bits,
    reach, found, status, cand_send, cand_recv, resp_send, resp_recv, tally, cnt_send, cnt_mid,
    recv_a, recv_b, in_sem, send_sem, recv_sem, sem_a, sem_b,
):
    depth, nx, ny = scores.shape
    chunks = ny // LANES
    steps = nx // SUB
    part_steps = steps // PARTS
    part_pairs = part_steps // 2
    group = math.gcd(GROUP, n)
    blocks = n // group
    me = lax.axis_index(AXIS)
    has = (me > 0, me < n - 1)
    lone = tuple(jnp.where(h, 0, 1).astype(jnp.int32) for h in has)
    columns = [slice(c * LANES, (c + 1) * LANES) for c in range(chunks)]

    def fetch(piece, z):
        return pltpu.make_async_copy(
            scores.at[z, :, columns[piece]], raw.at[piece, z], in_sem.at[piece, z]
        )

    for piece in range(chunks):
        for z in range(depth):
            fetch(piece, z).start()

    barrier = pltpu.get_barrier_semaphore()

    def greet(device):
        pl.semaphore_signal(
            barrier, inc=1, device_id=(device,), device_id_type=pl.DeviceIdType.MESH
        )

    place = lax.rem(me, group)
    base = me - place

    @pl.loop(1, group)
    def _(i):
        greet(base + lax.rem(place + i, group))

    @pl.loop(1, blocks)
    def _(i):
        greet(lax.rem(me + i * group, n))

    outside = (has[0] & (place == 0), has[1] & (place == group - 1))
    for side in range(2):

        @pl.when(outside[side])
        def _():
            greet(me + (1 if side else -1))

    tally[...] = jnp.zeros_like(tally)
    for side, mask in ((0, LOW), (1, HIGH)):

        @pl.when(jnp.logical_not(has[side]))
        def _():
            for phase in range(2):
                cand_recv[phase, side] = jnp.zeros(cand_recv.shape[2:], jnp.int32)
                resp_recv[phase, side] = jnp.full(
                    resp_recv.shape[2:], mask | mask << 16, jnp.int32
                )

    def wrap(ref, index):
        row = lax.broadcasted_iota(jnp.int32, (SUB, ny), 0)
        zero = jnp.zeros((SUB, ny), ref.dtype)
        for d in range(HALO):
            above = ref[index + (steps + d,)]
            ref[index + (d,)] = jnp.where(row == 0, zero, roll(above, 1, 0))
            below = ref[index + (HALO + d,)]
            ref[index + (HALO + steps + d,)] = jnp.where(
                row == SUB - 1, zero, roll(below, -1, 0)
            )

    def exchange(send, recv, phase, step, side, part, arrival):
        rows = pl.ds(part * part_pairs, part_pairs)
        there = arrival if arrival is not None else 1 - side
        return pltpu.make_async_remote_copy(
            src_ref=send.at[phase, side, rows],
            dst_ref=recv.at[phase, there, rows],
            send_sem=send_sem.at[step, side, part],
            recv_sem=recv_sem.at[step, there, part],
            device_id=(me + (1 if side else -1),),
            device_id_type=pl.DeviceIdType.MESH,
        )

    def start(send, recv, phase, step, part):
        for side in range(2):

            @pl.when(has[side])
            def _():
                exchange(send, recv, phase, step, side, part, None).start()

    def finish(send, recv, phase, step, part):
        for side in range(2):

            @pl.when(has[side])
            def _():
                exchange(send, recv, phase, step, side, part, None).wait_send()
                exchange(send, recv, phase, step, side, part, side).wait_recv()

    def turn(piece):
        for z in range(depth):
            for c in range(chunks):
                block = raw[piece, z, pl.ds(c, LANES, stride=chunks), :].T
                for half in range(LANES // steps):
                    turned[
                        z, c, pl.ds(piece * (LANES // steps) + half, steps, stride=SUB), :
                    ] = block[half * steps : (half + 1) * steps]

    def spot(c, k, z):
        return 8 + 4 * (c % 2) + 2 * (k % 2) + z % 2

    def widen(i):
        lane = lane_index()
        k = WIDENED * i
        for r in range(WIDENED):
            for z in range(depth):
                row = []
                for c in range(chunks):
                    score = turned[
                        z, c, pl.ds(pl.multiple_of(SUB * k, SUB) + SUB * r, SUB), :
                    ]
                    codes[z, k + r, :, columns[c]] = (score << 4) | spot(c, r, z)
                    value = encode(score)
                    field[z, k + r, :, columns[c]] = value
                    row.append(value)
                for c, v in enumerate(lanes5(row, jnp.maximum, lane)):
                    wide[z, k + (HALO + r), :, columns[c]] = v

    def search(phase, part):
        @pl.loop(0, part_pairs // 2)
        def _(i):
            k = part * part_steps + 4 * i
            small = [[[], []], [[], []]]
            for c in range(chunks):
                tall = [
                    rows5(lambda d: wide[z, k + (HALO + d), :, columns[c]], jnp.maximum)
                    for z in range(depth)
                ]
                best_code = ([], [])
                for r in range(4):
                    w = [tall[z][r] for z in range(depth)]
                    low, high = jnp.maximum(w[0], w[1]), jnp.maximum(w[2], w[3])
                    near[0, 0, k + r, :, columns[c]] = w[0]
                    near[0, 1, k + r, :, columns[c]] = low
                    near[1, 0, k + r, :, columns[c]] = high
                    near[1, 1, k + r, :, columns[c]] = w[3]
                    whole = jnp.maximum(low, high)
                    peak = [jnp.maximum(low, w[2]), whole, whole, jnp.maximum(w[1], high)]
                    best = [
                        field[z, k + r, :, columns[c]] == peak[z] for z in range(depth)
                    ]
                    own = [jnp.where(best[z], 4 << z, 0) for z in range(depth)]
                    found[k + r, :, columns[c]] = (own[0] | own[1]) | (own[2] | own[3])
                    for side in range(2):
                        a, b = 2 * side, 2 * side + 1
                        best_code[side].append(
                            jnp.where(
                                best[a],
                                codes[a, k + r, :, columns[c]],
                                jnp.where(best[b], codes[b, k + r, :, columns[c]], 0),
                            )
                        )
                for side in range(2):
                    for half in range(2):
                        small[side][half].append(
                            jnp.maximum(
                                best_code[side][2 * half], best_code[side][2 * half + 1]
                            )
                        )
            count = jnp.zeros((SUB, LANES), jnp.int32)
            for side in range(2):
                for half in range(2):
                    for c in range(chunks // 2):
                        v = jnp.maximum(*small[side][half][2 * c : 2 * c + 2])
                        cand_send[
                            phase, side, part * part_pairs + 2 * i + half, :, columns[c]
                        ] = v
                        if phase:
                            count = count + jnp.where(v > 0, lone[side], 0)
            if phase:
                tally[2] += count

    def judge(phase, part):
        @pl.loop(0, part_pairs // JUDGED)
        def _(i):
            count = jnp.zeros((SUB, LANES), jnp.int32)
            first = part * part_pairs + JUDGED * i
            for j in range(JUDGED):
                k = 2 * first + 2 * j
                halo = [[0] * chunks, [0] * chunks]
                for side, answer in ((0, HIGH), (1, LOW)):
                    verdicts = []
                    for p in range(chunks // 2):
                        code = cand_recv[phase, side, first + j, :, columns[p]]
                        plane = (code & 1) != 0
                        row = (code & 2) != 0
                        odd = (code & 4) != 0
                        bar = [
                            [
                                jnp.where(
                                    plane,
                                    near[side, 1, k + r, :, columns[2 * p + c]],
                                    near[side, 0, k + r, :, columns[2 * p + c]],
                                )
                                for r in range(2)
                            ]
                            for c in range(2)
                        ]
                        bar = [jnp.where(row, b[1], b[0]) for b in bar]
                        alive = (encode(code >> 4) > jnp.where(odd, bar[1], bar[0])) & (
                            code > 0
                        )
                        verdicts.append(jnp.where(alive, answer, 0))
                        if phase:
                            count = count + jnp.where(alive, 1, 0)
                            continue
                        bit = jnp.where(
                            alive, jnp.where(plane, 2 << (6 * side), 1 << (6 * side)), 0
                        )
                        for c, half in enumerate(
                            (jnp.where(odd, 0, bit), jnp.where(odd, bit, 0))
                        ):
                            halo[0][2 * p + c] |= jnp.where(row, 0, half)
                            halo[1][2 * p + c] |= jnp.where(row, half, 0)
                    resp_send[phase, side, first + j] = verdicts[0] | (verdicts[1] << 16)
                if not phase:
                    for r in range(2):
                        for c in range(chunks):
                            bits[k + r, :, columns[c]] = halo[r][c]
            if phase:
                tally[2] += count

    def allowed(phase, pair):
        word = resp_recv[phase, 0, pair] | resp_recv[phase, 1, pair]
        return word & 0xFFFF, word >> 16

    def settle(part):
        @pl.loop(0, part_pairs // JUDGED)
        def _(i):
            lane = lane_index()
            first = part * part_pairs + JUDGED * i
            for j in range(JUDGED):
                masks = allowed(0, first + j)
                for r in range(2):
                    k = 2 * first + (2 * j + r)
                    row = []
                    for c in range(chunks):
                        row.append(
                            bits[k, :, columns[c]] | (found[k, :, columns[c]] & masks[c // 2])
                        )
                        bits[k, :, columns[c]] = row[c]
                    for c, v in enumerate(lanes5(row, jnp.bitwise_or, lane)):
                        reach[k + HALO, :, columns[c]] = v

    def remove(part):
        @pl.loop(0, part_pairs // 2)
        def _(i):
            lane = lane_index()
            k = part * part_steps + 4 * i
            tall = [
                rows5(lambda d: reach[k + (HALO + d), :, columns[c]], jnp.bitwise_or)
                for c in range(chunks)
            ]
            first, second = tally[0], tally[1]
            for r in range(4):
                rows = [[] for _ in range(depth)]
                for c in range(chunks):
                    own = bits[k + r, :, columns[c]] & (LOW | HIGH)
                    held = tall[c][r]
                    two = held | (held >> 1)
                    cover = (two | (two >> 2) | (held >> 4)) & 15
                    status[c, pl.ds(pl.multiple_of(SUB * k, SUB) + SUB * r, SUB), :] = cover | (
                        own << 2
                    )
                    first = first + lax.population_count(own)
                    second = second + lax.population_count(cover)
                    for z in range(depth):
                        gone = (cover & (1 << z)) != 0
                        value = jnp.where(gone, 0.0, field[z, k + r, :, columns[c]])
                        field[z, k + r, :, columns[c]] = value
                        codes[z, k + r, :, columns[c]] = jnp.where(
                            gone, 0, codes[z, k + r, :, columns[c]]
                        )
                        rows[z].append(value)
                for z in range(depth):
                    for c, v in enumerate(lanes5(rows[z], jnp.maximum, lane)):
                        wide[z, k + (HALO + r), :, columns[c]] = v
            tally[0] = first
            tally[1] = second

    def final(part):
        @pl.loop(0, part_pairs // JUDGED)
        def _(i):
            first = part * part_pairs + JUDGED * i
            for j in range(JUDGED):
                masks = allowed(1, first + j)
                for r in range(2):
                    k = 2 * first + (2 * j + r)
                    for c in range(chunks):
                        at = pl.ds(pl.multiple_of(SUB * k, SUB), SUB)
                        held = status[c, at, :]
                        late = ((found[k, :, columns[c]] & masks[c // 2]) << 2) & ~(held << 4)
                        root = ((held | late) >> 4) & 15
                        both = root | ((held & 15 & ~root) << 8)
                        both = (both | (both << 2)) & 0x3333
                        both = (both | (both << 1)) & 0x5555
                        status[c, at, :] = (both & 0xFF) | (both >> 7)

    def offer(phase, part):
        search(phase, part)
        start(cand_send, cand_recv, phase, 2 * phase, part)

    def answer(phase, part):
        finish(cand_send, cand_recv, phase, 2 * phase, part)
        judge(phase, part)
        start(resp_send, resp_recv, phase, 2 * phase + 1, part)

    def confirm(part):
        finish(resp_send, resp_recv, 0, 1, part)
        settle(part)

    @pl.loop(0, chunks)
    def _(piece):
        for z in range(depth):
            pltpu.make_async_copy(
                scores.at[z, :, columns[0]], raw.at[piece, z], in_sem.at[piece, z]
            ).wait()
        turn(piece)

    @pl.loop(0, steps // WIDENED)
    def _(i):
        widen(i)

    for z in range(depth):
        wrap(wide, (z,))

    pl.semaphore_wait(
        barrier,
        group
        + blocks
        - 2
        + outside[0].astype(jnp.int32)
        + outside[1].astype(jnp.int32),
    )

    @pl.loop(1, PARTS + 1)
    def _(part):
        offer(0, lax.rem(part, PARTS))

    @pl.loop(1, PARTS + 1)
    def _(part):
        answer(0, lax.rem(part, PARTS))

    @pl.loop(1, PARTS)
    def _(part):
        confirm(part)

    remove(2)
    confirm(0)
    wrap(reach, ())

    @pl.loop(3, 6)
    def _(part):
        remove(lax.rem(part, PARTS))

    for z in range(depth):
        wrap(wide, (z,))

    @pl.loop(3, PARTS + 3)
    def _(part):
        offer(1, lax.rem(part, PARTS))

    @pl.loop(3, PARTS + 3)
    def _(part):
        answer(1, lax.rem(part, PARTS))

    roots, covered, late = (jnp.sum(tally[i]) for i in range(3))
    cells = depth * nx * ny
    column = lax.broadcasted_iota(jnp.int32, (1, LANES), 1)
    mine = jnp.where(
        column == 0,
        cells - roots,
        jnp.where(column == 1, cells - covered, cells - covered - late),
    )
    cnt_send[...] = mine

    def gather(send, recv, sems, i, device):
        return pltpu.make_async_remote_copy(
            src_ref=send,
            dst_ref=recv.at[i],
            send_sem=sems.at[0, i],
            recv_sem=sems.at[1, i],
            device_id=(device,),
            device_id_type=pl.DeviceIdType.MESH,
        )

    def near_by(i):
        return gather(cnt_send, recv_a, sem_a, i, base + lax.rem(place + i, group))

    def far_off(i):
        return gather(cnt_mid, recv_b, sem_b, i, lax.rem(me + i * group, n))

    @pl.loop(1, group)
    def _(i):
        near_by(i).start()

    def present(c):
        for piece in range(chunks):
            block = jnp.concatenate(
                [
                    status[
                        c, pl.ds(piece * (LANES // steps) + half, steps, stride=SUB), :
                    ]
                    for half in range(LANES // steps)
                ],
                axis=0,
            )
            packed_status[piece, pl.ds(c, LANES, stride=chunks), :] = block.T

    @pl.loop(1, group)
    def _(i):
        near_by(i).wait()

    subtotal = mine
    for i in range(1, group):
        subtotal = subtotal + recv_a[i]
    cnt_mid[...] = subtotal

    @pl.loop(1, blocks)
    def _(i):
        far_off(i).start()

    @pl.loop(3, PARTS + 3)
    def _(part):
        part = lax.rem(part, PARTS)
        finish(resp_send, resp_recv, 1, 3, part)
        final(part)

    for c in range(chunks):
        present(c)

    @pl.loop(1, blocks)
    def _(i):
        far_off(i).wait()

    total = subtotal
    for i in range(1, blocks):
        total = total + recv_b[i]
    counts[...] = total


def shards(scores):
    depth, nx, ny = scores.shape
    n = lax.axis_size(AXIS)
    group = math.gcd(GROUP, n)
    vmem = pltpu.VMEM
    steps = nx // SUB
    pairs = steps // 2
    packed_status, counts = pl.pallas_call(
        functools.partial(kernel, n),
        out_shape=(
            jax.ShapeDtypeStruct((ny // LANES, nx, LANES), jnp.int32),
            jax.ShapeDtypeStruct((1, LANES), jnp.int32),
        ),
        in_specs=[pl.BlockSpec(memory_space=pltpu.HBM)],
        out_specs=(pl.BlockSpec(memory_space=vmem),) * 2,
        scratch_shapes=[
            vmem((ny // LANES, depth, nx, LANES), jnp.int32),
            vmem((depth, ny // LANES, nx, LANES), jnp.int32),
            vmem((depth, steps, SUB, ny), jnp.int32),
            vmem((depth, steps, SUB, ny), jnp.float32),
            vmem((depth, steps + 2 * HALO, SUB, ny), jnp.float32),
            vmem((2, 2, steps, SUB, ny), jnp.float32),
            vmem((steps, SUB, ny), jnp.int32),
            vmem((steps + 2 * HALO, SUB, ny), jnp.int32),
            vmem((steps, SUB, ny), jnp.int32),
            vmem((ny // LANES, nx, LANES), jnp.int32),
            vmem((2, 2, pairs, SUB, ny // 2), jnp.int32),
            vmem((2, 2, pairs, SUB, ny // 2), jnp.int32),
            vmem((2, 2, pairs, SUB, ny // 4), jnp.int32),
            vmem((2, 2, pairs, SUB, ny // 4), jnp.int32),
            vmem((3, SUB, LANES), jnp.int32),
            vmem((1, LANES), jnp.int32),
            vmem((1, LANES), jnp.int32),
            vmem((group, 1, LANES), jnp.int32),
            vmem((n // group, 1, LANES), jnp.int32),
            pltpu.SemaphoreType.DMA((ny // LANES, depth)),
            pltpu.SemaphoreType.DMA((4, 2, PARTS)),
            pltpu.SemaphoreType.DMA((4, 2, PARTS)),
            pltpu.SemaphoreType.DMA((2, group)),
            pltpu.SemaphoreType.DMA((2, n // group)),
        ],
        compiler_params=pltpu.CompilerParams(
            collective_id=0, has_side_effects=True, vmem_limit_bytes=61 * 1024 * 1024
        ),
    )(scores)
    place = 2 * jnp.arange(depth, dtype=jnp.int32)[:, None, None]
    flat = jnp.concatenate([packed_status[p] for p in range(ny // LANES)], axis=1)
    return (flat[None] >> place) & 3, counts[0, :3]


def solution(mesh):
    return jax.shard_map(
        shards,
        mesh=mesh,
        in_specs=(P(AXIS, None, None),),
        out_specs=(P(AXIS, None, None), P()),
        check_vma=False,
    )
```

time: 60.9 us -> 45.3 us (0.74); the launches traced: 59.7 us -> 45.1 us
  Pallas kernels: 53.7 us -> 40 us
  local copies, waits for them, and re-layouts: 2.7 us -> 1.78 us
    pallas_call x1, Pallas kernels: 53.7 us -> 40 us  [shards(): pl.pallas_call(functools.partial(kernel, n), out_shape=(jax.ShapeDtypeStr...]
    unnamed x2, local copies, waits for them, and re-layouts: 2.18 us -> 0.01 us
    squeeze x1 -> x2, local copies, waits for them, and re-layouts: 0.51 us -> 1.77 us  [the longest x1 1.26 us: shards(): packed_status[p]]
where the time goes in v1:
time: 45.3 us; the launch traced here: 45.1 us
  Pallas kernels  40 us (88%)
  other arithmetic  2.69 us (6%)
  local copies, waits for them, and re-layouts  1.78 us (4%)
  between operations  0.67 us (1%)
    pallas_call x1, Pallas kernels, shards(): pl.pallas_call(functools.partial(kernel, n), out_shape=(jax.ShapeDtypeStr...  40 us
    and x1, other arithmetic, shards(): return (flat[None] >> place & 3, counts[0, :3])  2.62 us
    squeeze x1, local copies, waits for them, and re-layouts, shards(): packed_status[p]  1.26 us

profile of v1, /device:TPU:0, one launch (start us, length us, event | category | flops | bytes accessed | tf_op | source)
XLA Modules:
  0.0 45.1 jit_solution(6029817550729755602)
XLA Ops:
  0.6 40.0 %shard_map.30 = (s32[4,512,128]{2,1,0:T(8,128)}, s32[1,128]{1,0:T(1,128)}) custom-call(s32[4,512,512]{2,1,0:T(8,128)} %scores.1), custom_call_target="tpu_custom_call" | custom-call | tf_op jit(solution)/shard_map/pallas_call | solution.py:524
  40.6 0.0 copy-start
  40.6 1.3 %slice_bitcast_fusion.3 = (s32[512,128]{1,0:T(8,128)S(1)}, s32[512,128]{1,0:T(8,128)S(1)}, s32[512,128]{1,0:T(8,128)S(1)}, s32[512,128]{1,0:T(8,128)S(1)}) fusion(s32[4,512,128]{2,1,0:T(8,128)} %get-tuple-element.4), kind=kLoop, calls=%fused_computation.5 | loop fusion | bytes 2097152 | tf_op jit(solution)/shard_map/squeeze | solution.py:563
  41.9 0.1 pad_add_fusion
  42.0 0.0 copy-done
  42.0 0.5 %slice_bitcast_fusion.4 = s32[3]{0:T(128)} fusion(s32[1,128]{1,0:T(1,128)S(1)} %copy-done), kind=kLoop, calls=%fused_computation.6 | loop fusion | bytes 24 | tf_op jit(solution)/shard_map/squeeze | solution.py:564
  42.5 2.6 %shift-right-arithmetic_and_fusion = s32[4,512,512]{2,1,0:T(8,128)} fusion(s32[4]{0:T(128)S(1)} %iota_multiply_fusion, s32[512,512]{1,0:T(8,128)S(1)} %pad_add_fusion), kind=kLoop, calls=%fused_computation | loop fusion | flops 2097152 | bytes 5242896 | tf_op jit(solution)/shard_map/and | solution.py:564
  (1 shorter events, 0.0 us)
Async XLA Ops:
  40.6 1.4 %copy-start = (s32[1,128]{1,0:T(1,128)S(1)}, s32[1,128]{1,0:T(1,128)}, u32[]{:S(2)}) copy-start(s32[1,128]{1,0:T(1,128)} %get-tuple-element.5) | copy-start | bytes 1540

commit v2 on v1

--- a/solution.py
+++ b/solution.py
@@ -12,11 +12,11 @@
 AXIS = "gz"
 SUB = 8
 LANES = 128
-PARTS = 4
+PARTS = 8
 HALO = 2
 GROUP = 8
 JUDGED = 4
-WIDENED = 8
+SPLIT = 32
 LOW = 0x0C
 HIGH = 0x30
 
@@ -63,8 +63,8 @@
 
 
 def kernel(
-    n, scores, packed_status, counts, raw, turned, codes, field, wide, near, bits,
-    reach, found, status, cand_send, cand_recv, resp_send, resp_recv, tally, cnt_send, cnt_mid,
+    n, scores, decided, counts, raw, turned, codes, field, wide, near, bits,
+    reach, found, status, flat, cand_send, cand_recv, resp_send, resp_recv, tally, cnt_send, cnt_mid,
     recv_a, recv_b, in_sem, send_sem, recv_sem, sem_a, sem_b,
 ):
     depth, nx, ny = scores.shape
@@ -174,10 +174,10 @@
     def spot(c, k, z):
         return 8 + 4 * (c % 2) + 2 * (k % 2) + z % 2
 
-    def widen(i):
+    def widen(part):
         lane = lane_index()
-        k = WIDENED * i
-        for r in range(WIDENED):
+        k = part * part_steps
+        for r in range(part_steps):
             for z in range(depth):
                 row = []
                 for c in range(chunks):
@@ -317,11 +317,11 @@
                     for c, v in enumerate(lanes5(row, jnp.bitwise_or, lane)):
                         reach[k + HALO, :, columns[c]] = v
 
-    def remove(part):
-        @pl.loop(0, part_pairs // 2)
+    def remove(begin, blocks_of_rows):
+        @pl.loop(0, blocks_of_rows)
         def _(i):
             lane = lane_index()
-            k = part * part_steps + 4 * i
+            k = lax.rem(begin + 4 * i, steps)
             tall = [
                 rows5(lambda d: reach[k + (HALO + d), :, columns[c]], jnp.bitwise_or)
                 for c in range(chunks)
@@ -392,13 +392,6 @@
             ).wait()
         turn(piece)
 
-    @pl.loop(0, steps // WIDENED)
-    def _(i):
-        widen(i)
-
-    for z in range(depth):
-        wrap(wide, (z,))
-
     pl.semaphore_wait(
         barrier,
         group
@@ -408,45 +401,57 @@
         + outside[1].astype(jnp.int32),
     )
 
+    @pl.loop(0, PARTS)
+    def _(part):
+        widen(part)
+
+        @pl.when(part >= 2)
+        def _():
+            offer(0, part - 1)
+
+    for z in range(depth):
+        wrap(wide, (z,))
+
+    @pl.loop(PARTS - 1, PARTS + 1)
+    def _(part):
+        offer(0, lax.rem(part, PARTS))
+
     @pl.loop(1, PARTS + 1)
     def _(part):
-        offer(0, lax.rem(part, PARTS))
-
-    @pl.loop(1, PARTS + 1)
-    def _(part):
         answer(0, lax.rem(part, PARTS))
 
     @pl.loop(1, PARTS)
     def _(part):
         confirm(part)
 
-    remove(2)
+        @pl.when(part >= 2)
+        def _():
+            remove(part * part_steps - 4, part_steps // 4)
+
+        @pl.when(part >= 3)
+        def _():
+            offer(1, part - 1)
+
     confirm(0)
     wrap(reach, ())
-
-    @pl.loop(3, 6)
-    def _(part):
-        remove(lax.rem(part, PARTS))
-
+    remove(steps - 4, part_steps // 4 + 2)
     for z in range(depth):
         wrap(wide, (z,))
 
-    @pl.loop(3, PARTS + 3)
+    @pl.loop(PARTS - 1, PARTS + 2)
     def _(part):
         offer(1, lax.rem(part, PARTS))
 
-    @pl.loop(3, PARTS + 3)
-    def _(part):
-        answer(1, lax.rem(part, PARTS))
-
-    roots, covered, late = (jnp.sum(tally[i]) for i in range(3))
     cells = depth * nx * ny
     column = lax.broadcasted_iota(jnp.int32, (1, LANES), 1)
-    mine = jnp.where(
-        column == 0,
-        cells - roots,
-        jnp.where(column == 1, cells - covered, cells - covered - late),
-    )
+    roots, covered = jnp.sum(tally[0]), jnp.sum(tally[1])
+    mine = jnp.where(column == 0, cells - roots, cells - covered)
+
+    @pl.loop(2, PARTS + 2)
+    def _(part):
+        answer(1, lax.rem(part, PARTS))
+
+    mine = mine - jnp.where(column == 2, jnp.sum(tally[2]), 0)
     cnt_send[...] = mine
 
     def gather(send, recv, sems, i, device):
@@ -480,7 +485,7 @@
                 ],
                 axis=0,
             )
-            packed_status[piece, pl.ds(c, LANES, stride=chunks), :] = block.T
+            flat[piece, pl.ds(c, LANES, stride=chunks), :] = block.T
 
     @pl.loop(1, group)
     def _(i):
@@ -495,7 +500,7 @@
     def _(i):
         far_off(i).start()
 
-    @pl.loop(3, PARTS + 3)
+    @pl.loop(2, PARTS + 2)
     def _(part):
         part = lax.rem(part, PARTS)
         finish(resp_send, resp_recv, 1, 3, part)
@@ -503,6 +508,15 @@
 
     for c in range(chunks):
         present(c)
+
+    @pl.loop(0, nx // SPLIT)
+    def _(i):
+        here = pl.ds(pl.multiple_of(i * SPLIT, SPLIT), SPLIT)
+        for piece in range(chunks):
+            word = flat[piece, here, :]
+            for z in range(depth):
+                decided[z, here, columns[piece]] = (word >> (2 * z)) & 3
+
 
     @pl.loop(1, blocks)
     def _(i):
@@ -521,10 +535,10 @@
     vmem = pltpu.VMEM
     steps = nx // SUB
     pairs = steps // 2
-    packed_status, counts = pl.pallas_call(
+    decided, counts = pl.pallas_call(
         functools.partial(kernel, n),
         out_shape=(
-            jax.ShapeDtypeStruct((ny // LANES, nx, LANES), jnp.int32),
+            jax.ShapeDtypeStruct((depth, nx, ny), jnp.int32),
             jax.ShapeDtypeStruct((1, LANES), jnp.int32),
         ),
         in_specs=[pl.BlockSpec(memory_space=pltpu.HBM)],
@@ -539,6 +553,7 @@
             vmem((steps, SUB, ny), jnp.int32),
             vmem((steps + 2 * HALO, SUB, ny), jnp.int32),
             vmem((steps, SUB, ny), jnp.int32),
+            vmem((ny // LANES, nx, LANES), jnp.int32),
             vmem((ny // LANES, nx, LANES), jnp.int32),
             vmem((2, 2, pairs, SUB, ny // 2), jnp.int32),
             vmem((2, 2, pairs, SUB, ny // 2), jnp.int32),
@@ -556,12 +571,10 @@
             pltpu.SemaphoreType.DMA((2, n // group)),
         ],
         compiler_params=pltpu.CompilerParams(
-            collective_id=0, has_side_effects=True, vmem_limit_bytes=61 * 1024 * 1024
+            collective_id=0, has_side_effects=True, vmem_limit_bytes=48 * 1024 * 1024
         ),
     )(scores)
-    place = 2 * jnp.arange(depth, dtype=jnp.int32)[:, None, None]
-    flat = jnp.concatenate([packed_status[p] for p in range(ny // LANES)], axis=1)
-    return (flat[None] >> place) & 3, counts[0, :3]
+    return decided, counts[0, :3]
 
 
 def solution(mesh):

time: 45.3 us -> 41.3 us (0.912)
  other arithmetic: 2.69 us -> 0 us
  Pallas kernels: 40 us -> 38 us
  local copies, waits for them, and re-layouts: 1.78 us -> 2.53 us
    and x1 -> x0, other arithmetic: 2.62 us -> none  [shards(): return (flat[None] >> place & 3, counts[0, :3])]
    unnamed x2 -> x1, local copies, waits for them, and re-layouts: 0.01 us -> 2.01 us
    pallas_call x1, Pallas kernels: 40 us -> 38 us  [shards(): pl.pallas_call(functools.partial(kernel, n), out_shape=(jax.ShapeDtypeStr...]
    squeeze x2 -> x1, local copies, waits for them, and re-layouts: 1.77 us -> 0.51 us  [shards(): return (decided, counts[0, :3])]
where the time goes in v2:
time: 41.3 us; the launch traced here: 41.2 us
  Pallas kernels  38 us (92%)
  local copies, waits for them, and re-layouts  2.53 us (6%)
  between operations  0.64 us (2%)
    pallas_call x1, Pallas kernels, shards(): pl.pallas_call(functools.partial(kernel, n), out_shape=(jax.ShapeDtypeStr...  38 us
    unnamed x1, local copies, waits for them, and re-layouts  2.01 us

profile of v2, /device:TPU:0, one launch (start us, length us, event | category | flops | bytes accessed | tf_op | source)
XLA Modules:
  0.0 41.2 jit_solution(16896008327981967847)
XLA Ops:
  0.6 38.0 %shard_map.30 = (s32[4,512,512]{2,1,0:T(8,128)S(1)}, s32[1,128]{1,0:T(1,128)S(1)}) custom-call(s32[4,512,512]{2,1,0:T(8,128)} %scores.1), custom_call_target="tpu_custom_call" | custom-call | tf_op jit(solution)/shard_map/pallas_call | solution.py:538
  38.6 0.5 %slice_bitcast_fusion = s32[3]{0:T(128)} fusion(s32[1,128]{1,0:T(1,128)S(1)} %get-tuple-element.5), kind=kLoop, calls=%fused_computation | loop fusion | bytes 24 | tf_op jit(solution)/shard_map/squeeze | solution.py:577
  39.1 2.0 %copy.4 = s32[4,512,512]{2,1,0:T(8,128)} copy(s32[4,512,512]{2,1,0:T(8,128)S(1)} %get-tuple-element.8) | data formatting | bytes 8388608

commit v3 on v2

--- a/solution.py
+++ b/solution.py
@@ -13,12 +13,17 @@
 SUB = 8
 LANES = 128
 PARTS = 8
+AHEAD = 6
 HALO = 2
 GROUP = 8
 JUDGED = 4
 SPLIT = 32
 LOW = 0x0C
 HIGH = 0x30
+BASE = 2.0**23
+PLANE = 2.0**16
+ROW = 2.0**32
+ODD = 2.0**64
 
 
 def roll(x, shift, axis):
@@ -63,7 +68,7 @@
 
 
 def kernel(
-    n, scores, decided, counts, raw, turned, codes, field, wide, near, bits,
+    n, scores, decided, counts, raw, turned, field, wide, near, bits,
     reach, found, status, flat, cand_send, cand_recv, resp_send, resp_recv, tally, cnt_send, cnt_mid,
     recv_a, recv_b, in_sem, send_sem, recv_sem, sem_a, sem_b,
 ):
@@ -119,7 +124,7 @@
         @pl.when(jnp.logical_not(has[side]))
         def _():
             for phase in range(2):
-                cand_recv[phase, side] = jnp.zeros(cand_recv.shape[2:], jnp.int32)
+                cand_recv[phase, side] = jnp.zeros(cand_recv.shape[2:], jnp.float32)
                 resp_recv[phase, side] = jnp.full(
                     resp_recv.shape[2:], mask | mask << 16, jnp.int32
                 )
@@ -171,9 +176,6 @@
                         z, c, pl.ds(piece * (LANES // steps) + half, steps, stride=SUB), :
                     ] = block[half * steps : (half + 1) * steps]
 
-    def spot(c, k, z):
-        return 8 + 4 * (c % 2) + 2 * (k % 2) + z % 2
-
     def widen(part):
         lane = lane_index()
         k = part * part_steps
@@ -184,7 +186,6 @@
                     score = turned[
                         z, c, pl.ds(pl.multiple_of(SUB * k, SUB) + SUB * r, SUB), :
                     ]
-                    codes[z, k + r, :, columns[c]] = (score << 4) | spot(c, r, z)
                     value = encode(score)
                     field[z, k + r, :, columns[c]] = value
                     row.append(value)
@@ -211,32 +212,30 @@
                     near[1, 1, k + r, :, columns[c]] = w[3]
                     whole = jnp.maximum(low, high)
                     peak = [jnp.maximum(low, w[2]), whole, whole, jnp.maximum(w[1], high)]
-                    best = [
-                        field[z, k + r, :, columns[c]] == peak[z] for z in range(depth)
+                    value = [field[z, k + r, :, columns[c]] for z in range(depth)]
+                    best = [value[z] == peak[z] for z in range(depth)]
+                    own = [
+                        jnp.where(best[z], 4 << z, jnp.where(best[z + 1], 8 << z, 0))
+                        for z in (0, 2)
                     ]
-                    own = [jnp.where(best[z], 4 << z, 0) for z in range(depth)]
-                    found[k + r, :, columns[c]] = (own[0] | own[1]) | (own[2] | own[3])
+                    found[k + r, :, columns[c]] = own[0] | own[1]
                     for side in range(2):
                         a, b = 2 * side, 2 * side + 1
                         best_code[side].append(
                             jnp.where(
-                                best[a],
-                                codes[a, k + r, :, columns[c]],
-                                jnp.where(best[b], codes[b, k + r, :, columns[c]], 0),
+                                best[a], value[a], jnp.where(best[b], value[b] * PLANE, 0.0)
                             )
                         )
                 for side in range(2):
                     for half in range(2):
-                        small[side][half].append(
-                            jnp.maximum(
-                                best_code[side][2 * half], best_code[side][2 * half + 1]
-                            )
-                        )
+                        lower, upper = best_code[side][2 * half : 2 * half + 2]
+                        small[side][half].append(jnp.maximum(lower, upper * ROW))
             count = jnp.zeros((SUB, LANES), jnp.int32)
             for side in range(2):
                 for half in range(2):
                     for c in range(chunks // 2):
-                        v = jnp.maximum(*small[side][half][2 * c : 2 * c + 2])
+                        even, odd = small[side][half][2 * c : 2 * c + 2]
+                        v = jnp.maximum(even * (1 / ODD), odd)
                         cand_send[
                             phase, side, part * part_pairs + 2 * i + half, :, columns[c]
                         ] = v
@@ -257,9 +256,12 @@
                     verdicts = []
                     for p in range(chunks // 2):
                         code = cand_recv[phase, side, first + j, :, columns[p]]
-                        plane = (code & 1) != 0
-                        row = (code & 2) != 0
-                        odd = (code & 4) != 0
+                        odd = code >= BASE
+                        code = jnp.where(odd, code, code * ODD)
+                        row = code >= BASE * ROW
+                        code = jnp.where(row, code * (1 / ROW), code)
+                        plane = code >= BASE * PLANE
+                        code = jnp.where(plane, code * (1 / PLANE), code)
                         bar = [
                             [
                                 jnp.where(
@@ -272,9 +274,7 @@
                             for c in range(2)
                         ]
                         bar = [jnp.where(row, b[1], b[0]) for b in bar]
-                        alive = (encode(code >> 4) > jnp.where(odd, bar[1], bar[0])) & (
-                            code > 0
-                        )
+                        alive = code > jnp.where(odd, bar[1], bar[0])
                         verdicts.append(jnp.where(alive, answer, 0))
                         if phase:
                             count = count + jnp.where(alive, 1, 0)
@@ -317,39 +317,37 @@
                     for c, v in enumerate(lanes5(row, jnp.bitwise_or, lane)):
                         reach[k + HALO, :, columns[c]] = v
 
-    def remove(begin, blocks_of_rows):
-        @pl.loop(0, blocks_of_rows)
+    def remove(begin, bodies):
+        @pl.loop(0, bodies)
         def _(i):
             lane = lane_index()
-            k = lax.rem(begin + 4 * i, steps)
-            tall = [
-                rows5(lambda d: reach[k + (HALO + d), :, columns[c]], jnp.bitwise_or)
-                for c in range(chunks)
-            ]
             first, second = tally[0], tally[1]
-            for r in range(4):
-                rows = [[] for _ in range(depth)]
-                for c in range(chunks):
-                    own = bits[k + r, :, columns[c]] & (LOW | HIGH)
-                    held = tall[c][r]
-                    two = held | (held >> 1)
-                    cover = (two | (two >> 2) | (held >> 4)) & 15
-                    status[c, pl.ds(pl.multiple_of(SUB * k, SUB) + SUB * r, SUB), :] = cover | (
-                        own << 2
-                    )
-                    first = first + lax.population_count(own)
-                    second = second + lax.population_count(cover)
+            for block in range(2):
+                k = lax.rem(begin + 8 * i + 4 * block, steps)
+                tall = [
+                    rows5(lambda d: reach[k + (HALO + d), :, columns[c]], jnp.bitwise_or)
+                    for c in range(chunks)
+                ]
+                for r in range(4):
+                    rows = [[] for _ in range(depth)]
+                    at = pl.ds(pl.multiple_of(SUB * k, SUB) + SUB * r, SUB)
+                    for c in range(chunks):
+                        own = bits[k + r, :, columns[c]] & (LOW | HIGH)
+                        held = tall[c][r]
+                        two = held | (held >> 1)
+                        cover = (two | (two >> 2) | (held >> 4)) & 15
+                        status[c, at, :] = cover | (own << 2)
+                        first = first + lax.population_count(own)
+                        second = second + lax.population_count(cover)
+                        for z in range(depth):
+                            value = jnp.where(
+                                (cover & (1 << z)) != 0, 0.0, field[z, k + r, :, columns[c]]
+                            )
+                            field[z, k + r, :, columns[c]] = value
+                            rows[z].append(value)
                     for z in range(depth):
-                        gone = (cover & (1 << z)) != 0
-                        value = jnp.where(gone, 0.0, field[z, k + r, :, columns[c]])
-                        field[z, k + r, :, columns[c]] = value
-                        codes[z, k + r, :, columns[c]] = jnp.where(
-                            gone, 0, codes[z, k + r, :, columns[c]]
-                        )
-                        rows[z].append(value)
-                for z in range(depth):
-                    for c, v in enumerate(lanes5(rows[z], jnp.maximum, lane)):
-                        wide[z, k + (HALO + r), :, columns[c]] = v
+                        for c, v in enumerate(lanes5(rows[z], jnp.maximum, lane)):
+                            wide[z, k + (HALO + r), :, columns[c]] = v
             tally[0] = first
             tally[1] = second
 
@@ -392,6 +390,10 @@
             ).wait()
         turn(piece)
 
+    @pl.loop(0, AHEAD)
+    def _(part):
+        widen(part)
+
     pl.semaphore_wait(
         barrier,
         group
@@ -401,32 +403,33 @@
         + outside[1].astype(jnp.int32),
     )
 
-    @pl.loop(0, PARTS)
+    @pl.loop(1, AHEAD - 1)
+    def _(part):
+        offer(0, part)
+
+    @pl.loop(AHEAD, PARTS)
     def _(part):
         widen(part)
+        offer(0, part - 1)
+
+    for z in range(depth):
+        wrap(wide, (z,))
+
+    @pl.loop(PARTS - 1, PARTS + 1)
+    def _(part):
+        offer(0, lax.rem(part, PARTS))
+
+    @pl.loop(1, PARTS + 1)
+    def _(part):
+        answer(0, lax.rem(part, PARTS))
+
+    @pl.loop(1, PARTS)
+    def _(part):
+        confirm(part)
 
         @pl.when(part >= 2)
         def _():
-            offer(0, part - 1)
-
-    for z in range(depth):
-        wrap(wide, (z,))
-
-    @pl.loop(PARTS - 1, PARTS + 1)
-    def _(part):
-        offer(0, lax.rem(part, PARTS))
-
-    @pl.loop(1, PARTS + 1)
-    def _(part):
-        answer(0, lax.rem(part, PARTS))
-
-    @pl.loop(1, PARTS)
-    def _(part):
-        confirm(part)
-
-        @pl.when(part >= 2)
-        def _():
-            remove(part * part_steps - 4, part_steps // 4)
+            remove(part * part_steps - 4, part_steps // 8)
 
         @pl.when(part >= 3)
         def _():
@@ -434,7 +437,7 @@
 
     confirm(0)
     wrap(reach, ())
-    remove(steps - 4, part_steps // 4 + 2)
+    remove(steps - 4, part_steps // 8 + 1)
     for z in range(depth):
         wrap(wide, (z,))
 
@@ -546,7 +549,6 @@
         scratch_shapes=[
             vmem((ny // LANES, depth, nx, LANES), jnp.int32),
             vmem((depth, ny // LANES, nx, LANES), jnp.int32),
-            vmem((depth, steps, SUB, ny), jnp.int32),
             vmem((depth, steps, SUB, ny), jnp.float32),
             vmem((depth, steps + 2 * HALO, SUB, ny), jnp.float32),
             vmem((2, 2, steps, SUB, ny), jnp.float32),
@@ -555,8 +557,8 @@
             vmem((steps, SUB, ny), jnp.int32),
             vmem((ny // LANES, nx, LANES), jnp.int32),
             vmem((ny // LANES, nx, LANES), jnp.int32),
-            vmem((2, 2, pairs, SUB, ny // 2), jnp.int32),
-            vmem((2, 2, pairs, SUB, ny // 2), jnp.int32),
+            vmem((2, 2, pairs, SUB, ny // 2), jnp.float32),
+            vmem((2, 2, pairs, SUB, ny // 2), jnp.float32),
             vmem((2, 2, pairs, SUB, ny // 4), jnp.int32),
             vmem((2, 2, pairs, SUB, ny // 4), jnp.int32),
             vmem((3, SUB, LANES), jnp.int32),

time: 41.3 us -> 39.6 us (0.959)
  Pallas kernels: 38 us -> 36.4 us
    pallas_call x1, Pallas kernels: 38 us -> 36.4 us  [shards(): pl.pallas_call(functools.partial(kernel, n), out_shape=(jax.ShapeDtypeStr...]
where the time goes in v3:
time: 39.6 us; the launch traced here: 39.5 us
  Pallas kernels  36.4 us (92%)
  local copies, waits for them, and re-layouts  2.53 us (6%)
  between operations  0.64 us (2%)
    pallas_call x1, Pallas kernels, shards(): pl.pallas_call(functools.partial(kernel, n), out_shape=(jax.ShapeDtypeStr...  36.4 us
    unnamed x1, local copies, waits for them, and re-layouts  2.01 us

profile of v3, /device:TPU:0, one launch (start us, length us, event | category | flops | bytes accessed | tf_op | source)
XLA Modules:
  0.0 39.5 jit_solution(16704960629657571661)
XLA Ops:
  0.6 36.4 %shard_map.30 = (s32[4,512,512]{2,1,0:T(8,128)S(1)}, s32[1,128]{1,0:T(1,128)S(1)}) custom-call(s32[4,512,512]{2,1,0:T(8,128)} %scores.1), custom_call_target="tpu_custom_call" | custom-call | tf_op jit(solution)/shard_map/pallas_call | solution.py:541
  37.0 0.5 %slice_bitcast_fusion = s32[3]{0:T(128)} fusion(s32[1,128]{1,0:T(1,128)S(1)} %get-tuple-element.5), kind=kLoop, calls=%fused_computation | loop fusion | bytes 24 | tf_op jit(solution)/shard_map/squeeze | solution.py:579
  37.5 2.0 %copy.4 = s32[4,512,512]{2,1,0:T(8,128)} copy(s32[4,512,512]{2,1,0:T(8,128)S(1)} %get-tuple-element.8) | data formatting | bytes 8388608

commit v4 on v3

--- a/solution.py
+++ b/solution.py
@@ -321,7 +321,6 @@
         @pl.loop(0, bodies)
         def _(i):
             lane = lane_index()
-            first, second = tally[0], tally[1]
             for block in range(2):
                 k = lax.rem(begin + 8 * i + 4 * block, steps)
                 tall = [
@@ -337,8 +336,6 @@
                         two = held | (held >> 1)
                         cover = (two | (two >> 2) | (held >> 4)) & 15
                         status[c, at, :] = cover | (own << 2)
-                        first = first + lax.population_count(own)
-                        second = second + lax.population_count(cover)
                         for z in range(depth):
                             value = jnp.where(
                                 (cover & (1 << z)) != 0, 0.0, field[z, k + r, :, columns[c]]
@@ -348,8 +345,6 @@
                     for z in range(depth):
                         for c, v in enumerate(lanes5(rows[z], jnp.maximum, lane)):
                             wide[z, k + (HALO + r), :, columns[c]] = v
-            tally[0] = first
-            tally[1] = second
 
     def final(part):
         @pl.loop(0, part_pairs // JUDGED)
@@ -444,6 +439,17 @@
     @pl.loop(PARTS - 1, PARTS + 2)
     def _(part):
         offer(1, lax.rem(part, PARTS))
+
+    @pl.loop(0, nx // SPLIT)
+    def _(i):
+        first, second = tally[0], tally[1]
+        for r in range(0, SPLIT, SUB):
+            at = pl.ds(pl.multiple_of(i * SPLIT, SPLIT) + r, SUB)
+            for c in range(chunks):
+                first = first + lax.population_count(status[c, at, :] >> 4)
+                second = second + lax.population_count(status[c, at, :] & 15)
+        tally[0] = first
+        tally[1] = second
 
     cells = depth * nx * ny
     column = lax.broadcasted_iota(jnp.int32, (1, LANES), 1)

time: 39.6 us -> 39.5 us (level)
  no operation moved by 1% of the time
where the time goes in v4:
time: 39.5 us; the launch traced here: 39.4 us
  Pallas kernels  36.3 us (92%)
  local copies, waits for them, and re-layouts  2.53 us (6%)
  between operations  0.64 us (2%)
    pallas_call x1, Pallas kernels, shards(): pl.pallas_call(functools.partial(kernel, n), out_shape=(jax.ShapeDtypeStr...  36.3 us
    unnamed x1, local copies, waits for them, and re-layouts  2.01 us

profile of v4, /device:TPU:0, one launch (start us, length us, event | category | flops | bytes accessed | tf_op | source)
XLA Modules:
  0.0 39.4 jit_solution(3562266941433516005)
XLA Ops:
  0.6 36.3 %shard_map.30 = (s32[4,512,512]{2,1,0:T(8,128)S(1)}, s32[1,128]{1,0:T(1,128)S(1)}) custom-call(s32[4,512,512]{2,1,0:T(8,128)} %scores.1), custom_call_target="tpu_custom_call" | custom-call | tf_op jit(solution)/shard_map/pallas_call | solution.py:547
  36.9 0.5 %slice_bitcast_fusion = s32[3]{0:T(128)} fusion(s32[1,128]{1,0:T(1,128)S(1)} %get-tuple-element.5), kind=kLoop, calls=%fused_computation | loop fusion | bytes 24 | tf_op jit(solution)/shard_map/squeeze | solution.py:585
  37.4 2.0 %copy.4 = s32[4,512,512]{2,1,0:T(8,128)} copy(s32[4,512,512]{2,1,0:T(8,128)S(1)} %get-tuple-element.8) | data formatting | bytes 8388608
